TPU v7x, 512 devices: a whole 4x4x16 slice. The times are simulated.
512 devices in a mesh: tm: 128 (over z, x, core), space: 4 (over y).
Axes of the slice: x: 4, y: 4, z: 16, core: 2. Of those that a mesh axis runs over, the one named last changes fastest.
Arguments:
- state: float32 [512, 16, 64, 128], P('tm', 'space'), may hold values from -6 to 6
- source: float32 [512, 16, 64, 128], P('tm', 'space'), may hold values from -6 to 6
- absorption: float32 [16, 64, 128], P('space'), may hold values from 0.05 to 0.5
Outputs:
- relaxed: float32 [512, 16, 64, 128], P('tm', 'space')
- coarse_residual: float32 [128, 16, 64, 128], P('tm', 'space')
- residual_norm: float32 [], replicated
All inputs are finite; a program needn't handle non-finite values.
Results may differ from a plain program's by a relative error of at most 0.0004.
Values sent between devices are 32-bit elements; how exact they have to be, the bound alone decides.
A program may use at most 64 MiB of HBM per device.

v0:
```python
import math
import jax
import jax.numpy as jnp
from jax import lax
from jax.sharding import Mesh
from jax.sharding import PartitionSpec as P

CF = 4
SWEEPS = 5
TM = ("tm_0", "tm_1", "tm_2")
TM_SPACE = ("tm_0", "tm_1", "tm_2", "space")
coupling = 4.0


def shifted(value, axis, by):
    count = lax.axis_size(axis)
    pairs = [(i, i + by) for i in range(count) if 0 <= i + by < count]
    return lax.ppermute(value, axis, pairs)


def laid_out(tiles, dim):
    shape = list(tiles.shape[1:])
    shape[dim] *= tiles.shape[0]
    return jnp.moveaxis(tiles, 0, dim).reshape(shape)


def sent_to_all(value, axis):
    count = lax.axis_size(axis)
    return lax.all_to_all(
        jnp.broadcast_to(value[None], (count, *value.shape)), axis, 0, 0, tiled=True
    )


def collect(value, axis, dim):
    return laid_out(sent_to_all(value, axis), dim)


def by_axis(value, axes):
    for axis in axes:
        value = lax.psum(value, axis)
    return value


def sweep_weights(count):
    spread = 6.0 * coupling / (1.0 + 6.0 * coupling)
    return [
        1.0 / (1.0 + spread * math.cos(math.pi * (2 * k + 1) / (2 * count))) for k in range(count)
    ]


def apply_inner(extended, diag):
    inner = extended[1:-1]
    sides = jnp.pad(inner, ((0, 0), (1, 1), (1, 1)))
    beside = extended[2:] + extended[:-2]
    beside = beside + sides[:, 2:, 1:-1] + sides[:, :-2, 1:-1]
    beside = beside + sides[:, 1:-1, 2:] + sides[:, 1:-1, :-2]
    return diag * inner - coupling * beside


def step_whole(rhs, diag_full):
    field = rhs / diag_full
    for weight in sweep_weights(SWEEPS):
        extended = jnp.pad(field, ((1, 1), (0, 0), (0, 0)))
        field = field + weight * (rhs - apply_inner(extended, diag_full)) / diag_full
    return field


def local(state, source, absorption):
    depth_cells = absorption.shape[0]
    offset = lax.axis_index("space") * depth_cells

    def previous(last):
        return shifted(last, TM, 1)

    stacked = jnp.concatenate([state[:1], source, absorption[None]], axis=0)
    gathered = collect(stacked, "space", 1)
    source_full = gathered[1 : CF + 1]
    diag_full = 1.0 + 6.0 * coupling + gathered[CF + 1]

    def own_layers(field):
        return lax.dynamic_slice_in_dim(field, offset, depth_cells, 0)

    def back_full(last):
        return collect(previous(own_layers(last)), "space", 0)

    points = [gathered[0]] + [None] * (CF - 1)

    def relax_full(points):
        for j in range(1, CF):
            points[j] = step_whole(points[j - 1], diag_full) + source_full[j]
        return points

    points = relax_full(points)
    points[0] = step_whole(back_full(points[-1]), diag_full) + source_full[0]
    points = relax_full(points)
    coarse_full = source_full[0] + step_whole(back_full(points[-1]), diag_full) - points[0]
    coarse_residual = own_layers(coarse_full)
    points = [own_layers(point) for point in points]
    residual_norm = by_axis(jnp.sum(coarse_residual * coarse_residual), TM_SPACE)
    relaxed = jnp.stack(points, axis=0)
    return (relaxed, coarse_residual[None], residual_norm)


def solution(mesh):
    finer = Mesh(
        mesh.devices.reshape(16, 4, 2, mesh.shape["space"]), ("tm_0", "tm_1", "tm_2", "space")
    )
    return jax.shard_map(
        local,
        mesh=finer,
        in_specs=(P(TM, "space", None, None), P(TM, "space", None, None), P("space", None, None)),
        out_specs=(P(TM, "space", None, None), P(TM, "space", None, None), P()),
        check_vma=False,
    )
```

profile of v0, /device:TPU:2, one launch (start us, length us, event | category | flops | bytes accessed | tf_op | source)
XLA Modules:
  0.0 163.6 jit_solution(5410816493156166296)
XLA Ops:
  0.6 0.9 slice.797
  1.5 1.2 pad_maximum_fusion
  2.7 2.1 %broadcast_in_dim.11 = f32[4,6,4,64,128]{4,3,2,1,0:T(8,128)} broadcast(f32[6,4,64,128]{3,2,1,0:T(8,128)S(1)} %pad_maximum_fusion), dimensions={1,2,3,4} | broadcast | bytes 3932160 | tf_op jit(solution)/shard_map/broadcast_in_dim | solution.py:30
  4.8 4.5 %all-to-all-start = ((f32[4,6,4,64,128]{4,3,2,1,0:T(8,128)}), f32[4,6,4,64,128]{4,3,2,1,0:T(8,128)S(1)}, u32[]{:S(2)}, u32[]{:S(2)}) async-start(f32[4,6,4,64,128]{4,3,2,1,0:T(8,128)} %broadcast_in_dim.11), calls=%async_computation | async-start | bytes 6291456 | tf_op jit(solution)/shard_map/all_to_all | solution.py:29
  9.2 37.6 %all-to-all-done = f32[4,6,4,64,128]{4,3,2,1,0:T(8,128)S(1)} async-done(((f32[4,6,4,64,128]{4,3,2,1,0:T(8,128)}), f32[4,6,4,64,128]{4,3,2,1,0:T(8,128)S(1)}, u32[]{:S(2)}, u32[]{:S(2)}) %all-to-all-start) | async-done | bytes 3145760 | tf_op jit(solution)/shard_map/all_to_all | solution.py:29
  46.8 0.4 fusion.441
  47.2 0.1 bitcast_divide_fusion.1
  47.3 0.4 fusion.10
  47.7 0.4 fusion.21
  48.2 0.4 fusion.31
  48.6 0.4 fusion.42
  49.1 0.5 bitcast_divide_fusion.7
  49.5 0.4 fusion.65
  49.9 0.4 fusion.76
  50.4 0.4 fusion.86
  50.8 0.4 fusion.97
  51.3 0.5 bitcast_divide_fusion.5
  51.7 0.4 fusion.120
  52.1 0.4 fusion.131
  52.6 0.4 fusion.141
  53.0 0.5 bitcast_multiply_fusion
  53.5 0.3 fusion.158
  53.8 0.1 fusion.430
  53.9 1.9 %collective-permute-start = (f32[4,64,128]{2,1,0:T(8,128)S(1)}, f32[4,64,128]{2,1,0:T(8,128)S(1)}, u32[]{:S(2)}, u32[]{:S(2)}) collective-permute-start(f32[4,64,128]{2,1,0:T(8,128)S(1)} %fusion.430), channel_id=1, source_target_pairs={{0,4},{4,8},{8,12},{12,16},{16,20},{20,24},{24,28},{28,32},{32,36}... | collective-permute-start | bytes 393224 | tf_op jit(solution)/shard_map/ppermute | solution.py:18
  55.8 4.4 %collective-permute-done = f32[4,64,128]{2,1,0:T(8,128)S(1)} collective-permute-done((f32[4,64,128]{2,1,0:T(8,128)S(1)}, f32[4,64,128]{2,1,0:T(8,128)S(1)}, u32[]{:S(2)}, u32[]{:S(2)}) %collective-permute-start) | collective-permute-done | bytes 131104 | tf_op jit(solution)/shard_map/ppermute | solution.py:18
  60.2 11.5 %all_to_all.15 = f32[4,4,64,128]{3,2,1,0:T(8,128)S(1)} all-to-all(f32[4,4,64,128]{3,2,1,0:T(8,128)S(1)} %broadcast_in_dim.12), channel_id=1, replica_groups=mesh['tm_0'=16,'tm_1'=4,'tm_2'=2,'space'=4] {'space'}, dimensions={0} | all-to-all | bytes 1048576 | tf_op jit(solution)/shard_map/all_to_all | solution.py:29
  71.7 0.1 bitcast_divide_fusion
  71.8 0.4 fusion.169
  72.2 0.4 fusion.180
  72.7 0.4 fusion.190
  73.1 0.4 fusion.201
  73.6 0.5 bitcast_divide_fusion.3
  74.0 0.4 fusion.224
  74.5 0.4 fusion.235
  74.9 0.4 fusion.245
  75.3 0.4 fusion.256
  75.8 0.4 bitcast_divide_fusion.6
  76.2 0.4 fusion.279
  76.7 0.4 fusion.290
  77.1 0.4 fusion.300
  77.5 0.4 fusion.311
  77.9 0.4 bitcast_divide_fusion.4
  78.4 0.4 fusion.334
  78.8 0.4 fusion.345
  79.3 0.4 fusion.355
  79.7 0.5 bitcast_multiply_fusion.1
  80.2 0.3 fusion.372
  80.5 0.1 dynamic-slice_bitcast_fusion.1
  80.6 1.9 %collective-permute-start.1 = (f32[4,64,128]{2,1,0:T(8,128)S(1)}, f32[4,64,128]{2,1,0:T(8,128)S(1)}, u32[]{:S(2)}, u32[]{:S(2)}) collective-permute-start(f32[4,64,128]{2,1,0:T(8,128)S(1)} %get-tuple-element.27), channel_id=1, source_target_pairs={{0,4},{4,8},{8,12},{12,16},{16,20},{20,24},{24,28},{28,32},{32,36}... | collective-permute-start | bytes 393224 | tf_op jit(solution)/shard_map/ppermute | solution.py:18
  82.5 4.4 %collective-permute-done.1 = f32[4,64,128]{2,1,0:T(8,128)S(1)} collective-permute-done((f32[4,64,128]{2,1,0:T(8,128)S(1)}, f32[4,64,128]{2,1,0:T(8,128)S(1)}, u32[]{:S(2)}, u32[]{:S(2)}) %collective-permute-start.1) | collective-permute-done | bytes 131104 | tf_op jit(solution)/shard_map/ppermute | solution.py:18
  86.9 11.2 %all_to_all.16 = f32[4,4,64,128]{3,2,1,0:T(8,128)S(1)} all-to-all(f32[4,4,64,128]{3,2,1,0:T(8,128)S(1)} %broadcast_in_dim.13), channel_id=1, replica_groups=mesh['tm_0'=16,'tm_1'=4,'tm_2'=2,'space'=4] {'space'}, dimensions={0} | all-to-all | bytes 1048576 | tf_op jit(solution)/shard_map/all_to_all | solution.py:29
  98.1 0.1 bitcast_divide_fusion.2
  98.2 0.4 fusion.383
  98.7 0.4 fusion.394
  99.1 0.4 fusion.404
  99.6 0.4 fusion.415
  100.0 0.3 fusion.422
  100.4 1.3 multiply_reduce_fusion
  101.7 37.1 %psum.28 = f32[]{:T(128)} all-reduce(f32[]{:T(128)} %get-tuple-element.3), channel_id=1, replica_groups=mesh['tm_0'=16,'tm_1'=4,'tm_2'=2,'space'=4] {'tm_0'}, use_global_device_ids=true, to_apply=%region_1.2 | all-reduce | flops 1 | bytes 8 | tf_op jit(solution)/shard_map/psum | solution.py:40
  138.8 11.4 %psum.29 = f32[]{:T(128)} all-reduce(f32[]{:T(128)} %psum.28), channel_id=1, replica_groups=mesh['tm_0'=16,'tm_1'=4,'tm_2'=2,'space'=4] {'tm_1'}, use_global_device_ids=true, to_apply=%region_2.3 | all-reduce | flops 1 | bytes 8 | tf_op jit(solution)/shard_map/psum | solution.py:40
  150.2 3.1 %psum.30 = f32[]{:T(128)} all-reduce(f32[]{:T(128)} %psum.29), channel_id=1, replica_groups=mesh['tm_0'=16,'tm_1'=4,'tm_2'=2,'space'=4] {'tm_2'}, use_global_device_ids=true, to_apply=%region_3.4 | all-reduce | flops 1 | bytes 8 | tf_op jit(solution)/shard_map/psum | solution.py:40
  153.3 9.5 %psum.31 = f32[]{:T(128)} all-reduce(f32[]{:T(128)} %psum.30), channel_id=1, replica_groups=mesh['tm_0'=16,'tm_1'=4,'tm_2'=2,'space'=4] {'space'}, use_global_device_ids=true, to_apply=%region_4.5 | all-reduce | flops 1 | bytes 8 | tf_op jit(solution)/shard_map/psum | solution.py:40
  162.8 0.8 pad_maximum_fusion.1
  (3 shorter events, 0.1 us)
Async XLA Ops:
  4.8 42.0 %all-to-all-start = ((f32[4,6,4,64,128]{4,3,2,1,0:T(8,128)}), f32[4,6,4,64,128]{4,3,2,1,0:T(8,128)S(1)}, u32[]{:S(2)}, u32[]{:S(2)}) async-start(f32[4,6,4,64,128]{4,3,2,1,0:T(8,128)} %broadcast_in_dim.11), calls=%async_computation | async-start | bytes 6291456 | tf_op jit(solution)/shard_map/all_to_all | solution.py:29
  53.9 6.3 %collective-permute-start = (f32[4,64,128]{2,1,0:T(8,128)S(1)}, f32[4,64,128]{2,1,0:T(8,128)S(1)}, u32[]{:S(2)}, u32[]{:S(2)}) collective-permute-start(f32[4,64,128]{2,1,0:T(8,128)S(1)} %fusion.430), channel_id=1, source_target_pairs={{0,4},{4,8},{8,12},{12,16},{16,20},{20,24},{24,28},{28,32},{32,36}... | collective-permute-start | bytes 393224 | tf_op jit(solution)/shard_map/ppermute | solution.py:18
  80.6 6.3 %collective-permute-start.1 = (f32[4,64,128]{2,1,0:T(8,128)S(1)}, f32[4,64,128]{2,1,0:T(8,128)S(1)}, u32[]{:S(2)}, u32[]{:S(2)}) collective-permute-start(f32[4,64,128]{2,1,0:T(8,128)S(1)} %get-tuple-element.27), channel_id=1, source_target_pairs={{0,4},{4,8},{8,12},{12,16},{16,20},{20,24},{24,28},{28,32},{32,36}... | collective-permute-start | bytes 393224 | tf_op jit(solution)/shard_map/ppermute | solution.py:18
where the time goes:
time: 164 us
  blocking collectives  83.8 us (51%)
  waiting for transfers between devices  46.3 us (28%)
  other arithmetic  21.2 us (13%)
  starting transfers between devices  8.3 us (5%)
  local copies, waits for them, and re-layouts  3.06 us (2%)
    psum x4, blocking collectives, by_axis(): value = lax.psum(value, axis)  61.1 us
    all_to_all x1, waiting for transfers between devices, sent_to_all(): lax.all_to_all(jnp.broadcast_to(value[None], (count, *value.shape)), axis...  37.6 us
    all_to_all x2, blocking collectives, sent_to_all(): lax.all_to_all(jnp.broadcast_to(value[None], (count, *value.shape)), axis...  22.7 us
    add x30, other arithmetic, step_whole(): field + weight * (rhs - apply_inner(extended, diag_full)) / diag_full  12.9 us
    ppermute x2, waiting for transfers between devices, shifted(): return lax.ppermute(value, axis, pairs)  8.72 us
    all_to_all x1, starting transfers between devices, sent_to_all(): lax.all_to_all(jnp.broadcast_to(value[None], (count, *value.shape)), axis...  4.46 us
    ppermute x2, starting transfers between devices, shifted(): return lax.ppermute(value, axis, pairs)  3.84 us
  transfers between devices with their start and end apart: 3, of which 3 were waited for; matrix products, arithmetic and copies ran while one was open for 0% of the time, Pallas kernels for 0%

commit v1 on v0

--- a/solution.py
+++ b/solution.py
@@ -37,7 +37,12 @@
 
 def by_axis(value, axes):
     for axis in axes:
-        value = lax.psum(value, axis)
+
+        def store_weights_on(here_x, comm_axis):
+            passed = lax.all_gather(here_x, axis_name=comm_axis).sum(axis=0)
+            return passed
+
+        value = store_weights_on(value, axis)
     return value
 
 

time: 164 us -> 176 us (1.073)
  blocking collectives: 83.8 us -> 70.1 us
  local copies, waits for them, and re-layouts: 3.06 us -> 14.6 us
  waiting for transfers between devices: 46.3 us -> 52.8 us
  other arithmetic: 21.2 us -> 25.2 us
  starting transfers between devices: 8.3 us -> 11.9 us
    psum x4 -> x0, blocking collectives: 61.1 us -> none  [by_axis(): value = lax.psum(value, axis)]
    unnamed x0 -> x4, blocking collectives: none -> 58.6 us
    all_to_all x2 -> x1, blocking collectives: 22.7 us -> 11.5 us  [sent_to_all(): lax.all_to_all(jnp.broadcast_to(value[None], (count, *value.shape)), axis...]
    unnamed x0 -> x12, local copies, waits for them, and re-layouts: none -> 10.7 us
    all_to_all x1 -> x2, waiting for transfers between devices: 37.6 us -> 44 us  [sent_to_all(): lax.all_to_all(jnp.broadcast_to(value[None], (count, *value.shape)), axis...]
    all_to_all x1 -> x2, starting transfers between devices: 4.46 us -> 8.11 us  [sent_to_all(): lax.all_to_all(jnp.broadcast_to(value[None], (count, *value.shape)), axis...]
    reduce_sum x0 -> x4, other arithmetic: none -> 2.41 us  [store_weights_on(): passed = lax.all_gather(here_x, axis_name=comm_axis).sum(axis=0)]
  transfers between devices with their start and end apart: 3 -> 4, of which waited for: 3 -> 4; matrix products, arithmetic and copies ran while one was open for 0% -> 1% of each run, Pallas kernels for 0% -> 0%
where the time goes in v1:
time: 176 us
  blocking collectives  70.1 us (40%)
  waiting for transfers between devices  52.8 us (30%)
  other arithmetic  25.2 us (14%)
  local copies, waits for them, and re-layouts  14.6 us (8%)
  starting transfers between devices  11.9 us (7%)
    unnamed x4, blocking collectives  58.6 us
    all_to_all x2, waiting for transfers between devices, sent_to_all(): lax.all_to_all(jnp.broadcast_to(value[None], (count, *value.shape)), axis...  44 us
    add x30, other arithmetic, step_whole(): field + weight * (rhs - apply_inner(extended, diag_full)) / diag_full  12.8 us
    all_to_all x1, blocking collectives, sent_to_all(): lax.all_to_all(jnp.broadcast_to(value[None], (count, *value.shape)), axis...  11.5 us
    unnamed x12, local copies, waits for them, and re-layouts  10.7 us
    ppermute x2, waiting for transfers between devices, shifted(): return lax.ppermute(value, axis, pairs)  8.72 us
    all_to_all x2, starting transfers between devices, sent_to_all(): lax.all_to_all(jnp.broadcast_to(value[None], (count, *value.shape)), axis...  8.11 us
    ppermute x2, starting transfers between devices, shifted(): return lax.ppermute(value, axis, pairs)  3.84 us
  transfers between devices with their start and end apart: 4, of which 4 were waited for; matrix products, arithmetic and copies ran while one was open for 1% of the time, Pallas kernels for 0%

profile of v1, /device:TPU:2, one launch (start us, length us, event | category | flops | bytes accessed | tf_op | source)
XLA Modules:
  0.0 175.6 jit_solution(16651773811319763876)
XLA Ops:
  0.6 0.9 slice.797
  1.5 1.2 pad_maximum_fusion
  2.7 2.1 %broadcast_in_dim.11 = f32[4,6,4,64,128]{4,3,2,1,0:T(8,128)} broadcast(f32[6,4,64,128]{3,2,1,0:T(8,128)S(1)} %pad_maximum_fusion), dimensions={1,2,3,4} | broadcast | bytes 3932160 | tf_op jit(solution)/shard_map/broadcast_in_dim | solution.py:30
  4.8 4.6 %all-to-all-start = ((f32[4,6,4,64,128]{4,3,2,1,0:T(8,128)}), f32[4,6,4,64,128]{4,3,2,1,0:T(8,128)}, u32[]{:S(2)}, u32[]{:S(2)}) async-start(f32[4,6,4,64,128]{4,3,2,1,0:T(8,128)} %broadcast_in_dim.11), calls=%async_computation | async-start | bytes 6291456 | tf_op jit(solution)/shard_map/all_to_all | solution.py:29
  9.5 37.9 %all-to-all-done = f32[4,6,4,64,128]{4,3,2,1,0:T(8,128)} async-done(((f32[4,6,4,64,128]{4,3,2,1,0:T(8,128)}), f32[4,6,4,64,128]{4,3,2,1,0:T(8,128)}, u32[]{:S(2)}, u32[]{:S(2)}) %all-to-all-start) | async-done | bytes 3145760 | tf_op jit(solution)/shard_map/all_to_all | solution.py:29
  47.4 2.1 %fusion.441 = (f32[1,4,4,64,128]{4,3,2,0,1:T(8,128)S(1)}, f32[1,4,4,64,128]{4,3,2,0,1:T(8,128)S(1)}, f32[1,4,4,64,128]{4,3,2,0,1:T(8,128)S(1)}, f32[1,4,4,64,128...) fusion(f32[6,4,4,64,128]{4,3,2,0,1:T(8,128)} %bitcast.1), kind=kLoop, calls=%fused_computation.698 | loop fusion | flops 131072 | bytes 6291456 | tf_op jit(solution)/shard_map/slice | solution.py:95
  49.6 0.4 fusion.10
  50.0 0.4 fusion.21
  50.5 0.4 fusion.31
  50.9 0.4 fusion.42
  51.3 0.5 bitcast_divide_fusion.7
  51.8 0.4 fusion.65
  52.2 0.4 fusion.76
  52.7 0.4 fusion.86
  53.1 0.4 fusion.97
  53.6 0.5 bitcast_divide_fusion.5
  54.0 0.4 fusion.120
  54.5 0.4 fusion.131
  54.9 0.4 fusion.141
  55.4 0.5 bitcast_multiply_fusion
  56.3 1.9 %collective-permute-start = (f32[4,64,128]{2,1,0:T(8,128)S(1)}, f32[4,64,128]{2,1,0:T(8,128)S(1)}, u32[]{:S(2)}, u32[]{:S(2)}) collective-permute-start(f32[4,64,128]{2,1,0:T(8,128)S(1)} %fusion.430), channel_id=1, source_target_pairs={{0,4},{4,8},{8,12},{12,16},{16,20},{20,24},{24,28},{28,32},{32,36}... | collective-permute-start | bytes 393224 | tf_op jit(solution)/shard_map/ppermute | solution.py:18
  58.2 4.4 %collective-permute-done = f32[4,64,128]{2,1,0:T(8,128)S(1)} collective-permute-done((f32[4,64,128]{2,1,0:T(8,128)S(1)}, f32[4,64,128]{2,1,0:T(8,128)S(1)}, u32[]{:S(2)}, u32[]{:S(2)}) %collective-permute-start) | collective-permute-done | bytes 131104 | tf_op jit(solution)/shard_map/ppermute | solution.py:18
  62.6 11.5 %all_to_all.15 = f32[4,4,64,128]{3,2,1,0:T(8,128)S(1)} all-to-all(f32[4,4,64,128]{3,2,1,0:T(8,128)S(1)} %broadcast_in_dim.12), channel_id=1, replica_groups=mesh['tm_0'=16,'tm_1'=4,'tm_2'=2,'space'=4] {'space'}, dimensions={0} | all-to-all | bytes 1048576 | tf_op jit(solution)/shard_map/all_to_all | solution.py:29
  74.2 0.4 fusion.169
  74.6 0.4 fusion.180
  75.1 0.4 fusion.190
  75.5 0.4 fusion.201
  75.9 0.4 bitcast_divide_fusion.3
  76.8 0.4 fusion.235
  77.6 0.4 fusion.256
  78.1 0.4 bitcast_divide_fusion.6
  78.5 0.4 fusion.279
  78.9 0.4 fusion.290
  79.8 0.4 fusion.311
  80.2 0.4 bitcast_divide_fusion.4
  81.1 0.4 fusion.345
  81.9 0.5 bitcast_multiply_fusion.1
  82.8 1.9 %collective-permute-start.1 = (f32[4,64,128]{2,1,0:T(8,128)S(1)}, f32[4,64,128]{2,1,0:T(8,128)S(1)}, u32[]{:S(2)}, u32[]{:S(2)}) collective-permute-start(f32[4,64,128]{2,1,0:T(8,128)S(1)} %get-tuple-element.27), channel_id=1, source_target_pairs={{0,4},{4,8},{8,12},{12,16},{16,20},{20,24},{24,28},{28,32},{32,36}... | collective-permute-start | bytes 393224 | tf_op jit(solution)/shard_map/ppermute | solution.py:18
  84.8 4.4 %collective-permute-done.1 = f32[4,64,128]{2,1,0:T(8,128)S(1)} collective-permute-done((f32[4,64,128]{2,1,0:T(8,128)S(1)}, f32[4,64,128]{2,1,0:T(8,128)S(1)}, u32[]{:S(2)}, u32[]{:S(2)}) %collective-permute-start.1) | collective-permute-done | bytes 131104 | tf_op jit(solution)/shard_map/ppermute | solution.py:18
  89.1 0.8 broadcast_in_dim.13
  90.0 3.5 %all-to-all-start.2 = ((f32[4,4,64,128]{3,2,1,0:T(8,128)}), f32[4,4,64,128]{3,2,1,0:T(8,128)S(1)}, u32[]{:S(2)}, u32[]{:S(2)}) async-start(f32[4,4,64,128]{3,2,1,0:T(8,128)} %broadcast_in_dim.13), calls=%async_computation.2 | async-start | bytes 1048576 | tf_op jit(solution)/shard_map/all_to_all | solution.py:29
  93.4 1.3 dynamic-slice
  94.8 1.3 dynamic-slice.1
  96.1 6.1 %all-to-all-done.2 = f32[4,4,64,128]{3,2,1,0:T(8,128)S(1)} async-done(((f32[4,4,64,128]{3,2,1,0:T(8,128)}), f32[4,4,64,128]{3,2,1,0:T(8,128)S(1)}, u32[]{:S(2)}, u32[]{:S(2)}) %all-to-all-start.2) | async-done | bytes 524320 | tf_op jit(solution)/shard_map/all_to_all | solution.py:29
  102.3 0.4 fusion.383
  102.7 0.4 fusion.394
  103.1 0.4 fusion.404
  103.6 0.4 fusion.415
  104.4 1.3 multiply_reduce_fusion
  105.7 1.4 dynamic-update-slice
  107.1 36.5 %all-reduce.80 = f32[16]{0:T(128)S(1)} all-reduce(f32[16]{0:T(128)S(1)} %dynamic-update-slice), channel_id=1, replica_groups=mesh['tm_0'=16,'tm_1'=4,'tm_2'=2,'space'=4] {'tm_0'}, use_global_device_ids=true, to_apply=%add.80 | all-reduce | flops 16 | bytes 128
  143.6 0.6 reduce_sum.46
  144.2 1.3 dynamic-update-slice.1
  145.5 1.3 dynamic-slice.2
  146.8 10.7 %all-reduce.81 = f32[4]{0:T(128)S(1)} all-reduce(f32[4]{0:T(128)S(1)} %dynamic-update-slice.1), channel_id=1, replica_groups=mesh['tm_0'=16,'tm_1'=4,'tm_2'=2,'space'=4] {'tm_1'}, use_global_device_ids=true, to_apply=%add.81 | all-reduce | flops 4 | bytes 32
  157.5 0.6 reduce_sum.47
  158.1 1.4 dynamic-update-slice.2
  159.5 1.3 dynamic-slice.3
  160.8 2.4 %all-reduce.82 = f32[2]{0:T(128)S(1)} all-reduce(f32[2]{0:T(128)S(1)} %dynamic-update-slice.2), channel_id=1, replica_groups=mesh['tm_0'=16,'tm_1'=4,'tm_2'=2,'space'=4] {'tm_2'}, use_global_device_ids=true, to_apply=%add.82 | all-reduce | flops 2 | bytes 16
  163.2 0.6 reduce_sum.48
  163.8 1.4 dynamic-update-slice.3
  165.3 8.9 %all-reduce.83 = f32[4]{0:T(128)S(1)} all-reduce(f32[4]{0:T(128)S(1)} %dynamic-update-slice.3), channel_id=1, replica_groups=mesh['tm_0'=16,'tm_1'=4,'tm_2'=2,'space'=4] {'space'}, use_global_device_ids=true, to_apply=%add.83 | all-reduce | flops 4 | bytes 32
  174.2 0.6 reduce_sum.49
  174.8 0.8 pad_maximum_fusion.1
  (19 shorter events, 3.5 us)
Async XLA Ops:
  4.8 42.5 %all-to-all-start = ((f32[4,6,4,64,128]{4,3,2,1,0:T(8,128)}), f32[4,6,4,64,128]{4,3,2,1,0:T(8,128)}, u32[]{:S(2)}, u32[]{:S(2)}) async-start(f32[4,6,4,64,128]{4,3,2,1,0:T(8,128)} %broadcast_in_dim.11), calls=%async_computation | async-start | bytes 6291456 | tf_op jit(solution)/shard_map/all_to_all | solution.py:29
  56.3 6.3 %collective-permute-start = (f32[4,64,128]{2,1,0:T(8,128)S(1)}, f32[4,64,128]{2,1,0:T(8,128)S(1)}, u32[]{:S(2)}, u32[]{:S(2)}) collective-permute-start(f32[4,64,128]{2,1,0:T(8,128)S(1)} %fusion.430), channel_id=1, source_target_pairs={{0,4},{4,8},{8,12},{12,16},{16,20},{20,24},{24,28},{28,32},{32,36}... | collective-permute-start | bytes 393224 | tf_op jit(solution)/shard_map/ppermute | solution.py:18
  82.8 6.3 %collective-permute-start.1 = (f32[4,64,128]{2,1,0:T(8,128)S(1)}, f32[4,64,128]{2,1,0:T(8,128)S(1)}, u32[]{:S(2)}, u32[]{:S(2)}) collective-permute-start(f32[4,64,128]{2,1,0:T(8,128)S(1)} %get-tuple-element.27), channel_id=1, source_target_pairs={{0,4},{4,8},{8,12},{12,16},{16,20},{20,24},{24,28},{28,32},{32,36}... | collective-permute-start | bytes 393224 | tf_op jit(solution)/shard_map/ppermute | solution.py:18
  90.0 12.2 %all-to-all-start.2 = ((f32[4,4,64,128]{3,2,1,0:T(8,128)}), f32[4,4,64,128]{3,2,1,0:T(8,128)S(1)}, u32[]{:S(2)}, u32[]{:S(2)}) async-start(f32[4,4,64,128]{3,2,1,0:T(8,128)} %broadcast_in_dim.13), calls=%async_computation.2 | async-start | bytes 1048576 | tf_op jit(solution)/shard_map/all_to_all | solution.py:29
